TPU v7x, 256 devices: a whole 4x4x8 slice. The times are simulated.
256 devices in a mesh: ang: 32 (over y, z_hi, x), slab: 8 (over z_lo, core).
Axes of the slice: x: 4, y: 4, z: 8 (z_hi: 2, z_lo: 4; z = z_hi * 4 + z_lo), core: 2. Of those that a mesh axis runs over, the one named last changes fastest.
Arguments:
- updates: float32 [128, 2, 1024, 512], P('ang', None, 'slab'), may hold values from -6 to 6
- interp_tiles: bfloat16 [128, 32, 256, 128], P('ang'), may hold values from -0.25 to 0.25
- band_start: int32 [128, 32], P('ang'), may hold values from 0 to 2
- angle_id: int32 [128], P('ang'), may hold values from 0 to 127, each once
- angle_weight: float32 [128], replicated, may hold values from 0.05 to 0.5
- volume: float32 [4096, 2, 1024], P('ang', None, 'slab'), may hold values from -6 to 6
Outputs:
- volume_next: float32 [4096, 2, 1024], P('ang', None, 'slab')
- projection: float32 [128, 2, 1024, 512], P('ang', None, 'slab')
Inputs may be any that keep to these rules, and one draw needn't show every extreme that they name: Tile j of angle slot a reads detector columns 128 * band_start[a, j] up to 256 further. `angle_id`: each measured angle stands in exactly one slot.
All inputs are finite; a program needn't handle non-finite values.
Results may differ from a plain program's by a relative error of at most 0.0062.
Values may be sent and summed in bfloat16 or wider, within the bound.
A program may use at most 128 MiB of HBM per device.

v0:
```python
import jax
import jax.numpy as jnp
from jax import lax
from jax.sharding import PartitionSpec as P

SMOOTHING = 0.25


def extended(cells, sides, width):
    for axis, dim in sides:
        count = lax.axis_size(axis)
        ends = count - 1
        head = lax.slice_in_dim(cells, 0, width, axis=dim)
        tail = lax.slice_in_dim(cells, cells.shape[dim] - width, cells.shape[dim], axis=dim)
        cells = jnp.concatenate(
            [
                lax.ppermute(tail, axis, [(i, (i + 1) % count) for i in range(ends)]),
                cells,
                lax.ppermute(head, axis, [((i + 1) % count, i) for i in range(ends)]),
            ],
            axis=dim,
        )
    return cells


def cut_along(value, dim, devices):
    lengths = value.shape
    parts = value.reshape(*lengths[:dim], devices, lengths[dim] // devices, *lengths[dim + 1 :])
    return jnp.moveaxis(parts, dim, 0)


def sent_and_summed(value, axis, dim):
    parts = cut_along(value, dim, lax.axis_size(axis))
    arrived = lax.all_to_all(parts, axis, split_axis=0, concat_axis=0, tiled=True)
    return arrived.astype(jnp.float32).sum(axis=0)


def laid_out(parts, dim):
    parts = jnp.moveaxis(parts, 0, dim)
    lengths = parts.shape
    return parts.reshape(*lengths[:dim], lengths[dim] * lengths[dim + 1], *lengths[dim + 2 :])


def from_everyone(value, axis):
    copies = jnp.broadcast_to(value, (lax.axis_size(axis), *value.shape))
    return lax.all_to_all(copies, axis, split_axis=0, concat_axis=0, tiled=True)


def gathered_copies(value, axis, dim):
    return laid_out(from_everyone(value, axis), dim)


def clamp_absorption(field):
    channel = jnp.arange(2, dtype=jnp.int32)[None, :, None]
    return jnp.where(channel == 1, jnp.maximum(field, 0.0), field)


def shards(updates, interp_tiles, band_start, angle_id, angle_weight, volume):
    local_angles = updates.shape[0]
    slab_depth = updates.shape[2]
    detector = updates.shape[3]
    band_width = interp_tiles.shape[2]
    block_size = interp_tiles.shape[3]
    row_count = 2 * slab_depth
    position_count = detector // block_size - 1
    share = volume.shape[0]
    matches = angle_id[:, None] == jnp.arange(angle_weight.shape[0], dtype=jnp.int32)[None, :]
    chosen = jnp.sum(jnp.where(matches, angle_weight[None, :], 0.0), axis=1)
    scaled = (
        (chosen[:, None, None, None] * updates)
        .astype(jnp.bfloat16)
        .reshape(local_angles, row_count, detector)
    )
    stacked = jnp.stack(
        [
            lax.slice_in_dim(
                scaled, block_size * offset_index, block_size * offset_index + band_width, axis=2
            )
            for offset_index in range(position_count)
        ],
        axis=1,
    )
    positions = jnp.arange(position_count, dtype=jnp.int32)
    padded = extended(volume, (("slab", 2),), 1)
    smooth = volume - SMOOTHING * (2.0 * volume - padded[:, :, :-2] - padded[:, :, 2:])
    tile_part = interp_tiles
    start_part = band_start
    onehot = (start_part[:, :, None] == positions).astype(jnp.bfloat16)
    windows = jnp.einsum(
        "ajk,akrq->ajrq", onehot, stacked, preferred_element_type=jnp.float32
    ).astype(jnp.bfloat16)
    term = jnp.einsum("ajrq,ajqp->jpr", windows, tile_part, preferred_element_type=jnp.float32)
    summed = sent_and_summed(
        term.reshape(share * lax.axis_size("ang"), 2, slab_depth).astype(jnp.bfloat16), "ang", 0
    )
    volume_next = clamp_absorption(smooth + summed)
    piece = gathered_copies(volume_next.astype(jnp.bfloat16), "ang", 0)
    tile_count = piece.shape[0] // block_size
    tile_part = interp_tiles
    start_part = band_start
    images = jnp.einsum(
        "jpr,ajqp->ajrq",
        piece.reshape(tile_count, block_size, row_count),
        tile_part,
        preferred_element_type=jnp.float32,
    )
    onehot = (start_part[:, :, None] == positions).astype(jnp.float32)
    grouped = jnp.einsum("ajk,ajrq->akrq", onehot, images, precision=lax.Precision.HIGHEST)
    projection = jnp.zeros((local_angles, row_count, detector), jnp.float32)
    for offset_index in range(position_count):
        projection = projection + jnp.pad(
            grouped[:, offset_index],
            (
                (0, 0),
                (0, 0),
                (block_size * offset_index, detector - block_size * offset_index - band_width),
            ),
        )
    return (volume_next, projection.reshape(local_angles, 2, slab_depth, detector))


def solution(mesh):
    placed = (
        P("ang", None, "slab", None),
        P("ang", None, None, None),
        P("ang", None),
        P("ang"),
        P(),
        P("ang", None, "slab"),
    )
    return jax.shard_map(
        shards,
        mesh=mesh,
        in_specs=placed,
        out_specs=(P("ang", None, "slab"), P("ang", None, "slab", None)),
        check_vma=False,
    )
```

profile of v0, /device:TPU:2, one launch (start us, length us, event | category | flops | bytes accessed | tf_op | source)
XLA Modules:
  0.0 232.6 jit_solution(15859046963648792834)
XLA Ops:
  0.6 0.9 select_reduce_fusion
  1.5 1.9 multiply_convert_fusion
  3.4 0.1 slice_bitcast_fusion.2
  3.6 0.8 copy.73
  4.4 0.8 copy.75
  5.2 0.8 copy.74
  6.0 9.1 %convolution_convert_fusion = bf16[4,32,256,256]{3,1,2,0:T(8,128)(2,1)} fusion(bf16[4,1,256,256]{3,1,2,0:T(2,128)(2,1)S(1)} %copy.75, bf16[4,1,256,256]{3,1,2,0:T(2,128)(2,1)S(1)} %copy.74, bf16[4,1,256,256]{3,1,2,0:T(2,128)(2,1)S(1)} %copy.73, s32[4,32]{1,0:T(4,128)S(1)} %copy-done), kind=kOutput, calls=%fused_computation.5 | convolution fusion | flops 63439232 | bytes 18350592 | tf_op jit(solution)/shard_map/ajk,akrq->ajrq/dot_general | solution.py:89
  15.2 21.2 %bitcast_convert_fusion = bf16[32,256,128]{2,1,0:T(8,128)(2,1)} fusion(bf16[4,32,256,128]{3,2,1,0:T(8,128)(2,1)S(1)} %bitcast.36, bf16[4,32,256,256]{3,1,2,0:T(8,128)(2,1)} %convolution_convert_fusion), kind=kOutput, calls=%fused_computation.8 | convolution fusion | flops 2148532224 | bytes 27262976 | tf_op jit(solution)/shard_map/ajrq,ajqp->jpr/dot_general | solution.py:92
  36.3 14.4 %all-to-all-start = ((bf16[32,128,2,128]{1,3,2,0:T(8,128)(2,1)}), bf16[32,128,2,128]{1,3,2,0:T(8,128)(2,1)S(1)}, u32[]{:S(2)}, u32[]{:S(2)}) async-start(bf16[32,128,2,128]{1,3,2,0:T(8,128)(2,1)} %bitcast.40), calls=%async_computation | async-start | bytes 4194304 | tf_op jit(solution)/shard_map/all_to_all | solution.py:34
  50.7 0.1 copy.72
  50.8 1.3 collective-permute-start
  52.1 1.3 collective-permute-start.1
  53.5 50.3 %all-to-all-done = bf16[32,128,2,128]{1,3,2,0:T(8,128)(2,1)S(1)} async-done(((bf16[32,128,2,128]{1,3,2,0:T(8,128)(2,1)}), bf16[32,128,2,128]{1,3,2,0:T(8,128)(2,1)S(1)}, u32[]{:S(2)}, u32[]{:S(2)}) %all-to-all-start) | async-done | bytes 2097184 | tf_op jit(solution)/shard_map/all_to_all | solution.py:34
  103.7 0.3 convert_reduce_fusion
  104.1 0.1 fusion.26
  104.1 1.8 broadcast_in_dim.35
  106.0 5.1 %all-to-all-start.1 = ((bf16[32,128,2,128]{1,3,2,0:T(8,128)(2,1)}), bf16[32,128,2,128]{1,3,2,0:T(8,128)(2,1)S(1)}, u32[]{:S(2)}, u32[]{:S(2)}) async-start(bf16[32,128,2,128]{1,3,2,0:T(8,128)(2,1)} %broadcast_in_dim.35), calls=%async_computation.1 | async-start | bytes 4194304 | tf_op jit(solution)/shard_map/all_to_all | solution.py:46
  111.1 0.8 copy.82
  111.9 52.1 %all-to-all-done.1 = bf16[32,128,2,128]{1,3,2,0:T(8,128)(2,1)S(1)} async-done(((bf16[32,128,2,128]{1,3,2,0:T(8,128)(2,1)}), bf16[32,128,2,128]{1,3,2,0:T(8,128)(2,1)S(1)}, u32[]{:S(2)}, u32[]{:S(2)}) %all-to-all-start.1) | async-done | bytes 2097184 | tf_op jit(solution)/shard_map/all_to_all | solution.py:46
  164.0 19.0 %convolution_bitcast_fusion = f32[4,32,256,256]{3,2,0,1:T(8,128)} fusion(bf16[32,128,256,1]{1,2,3,0:T(8,128)(2,1)S(1)} %bitcast.37, bf16[4,32,256,128]{3,2,1,0:T(8,128)(2,1)} %param.7), kind=kOutput, calls=%fused_computation.4 | convolution fusion | flops 2147483648 | bytes 44040192 | tf_op jit(solution)/shard_map/jpr,ajqp->ajrq/dot_general | solution.py:101
  183.0 40.2 %fusion = f32[4,3,256,256]{3,1,2,0:T(4,128)} fusion(f32[4,32,256,256]{3,2,0,1:T(8,128)} %convolution_bitcast_fusion, s32[4,32]{1,0:T(4,128)S(1)} %copy-done), kind=kOutput, calls=%fused_computation | convolution fusion | flops 301990272 | bytes 36700672 | tf_op jit(solution)/shard_map/ajk,ajrq->akrq/dot_general | solution.py:108
  223.1 7.6 %fusion.27 = (f32[4,1,256,256]{3,1,2,0:T(1,128)S(1)}, f32[4,1,256,256]{3,1,2,0:T(1,128)S(1)}, f32[4,1,256,256]{3,1,2,0:T(1,128)S(1)}) fusion(f32[4,3,256,256]{3,1,2,0:T(4,128)} %fusion), kind=kLoop, calls=%fused_computation.40 | loop fusion | bytes 6291456 | tf_op jit(solution)/shard_map/slice | solution.py:112
  230.8 0.2 copy_bitcast_fusion
  231.0 1.6 pad_add_fusion
  (14 shorter events, 0.1 us)
Async XLA Ops:
  3.4 2.6 %copy-start = (s32[4,32]{1,0:T(4,128)S(1)}, s32[4,32]{1,0:T(4,128)}, u32[]{:S(2)}) copy-start(s32[4,32]{1,0:T(4,128)} %param.8) | copy-start | bytes 1540
  5.2 10.0 %slice-start = ((s8[8388608]{0:T(1024)(128)(4,1)}), s8[4194304]{0:T(1024)(128)(4,1)S(1)}, s32[]{:S(2)}) async-start(s8[8388608]{0:T(1024)(128)(4,1)} %bitcast.35), calls=%async_computation.2 | async-start | bytes 8388608
  6.0 9.1 %slice-start.1 = ((s8[8388608]{0:T(1024)(128)(4,1)}), s8[4194304]{0:T(1024)(128)(4,1)S(1)}, s32[]{:S(2)}) async-start(s8[8388608]{0:T(1024)(128)(4,1)} %bitcast.35), calls=%async_computation.3 | async-start | bytes 8388608
  36.3 14.4 %copy-start.1 = (f32[128,2,128]{2,1,0:T(2,128)S(1)}, f32[128,2,128]{2,1,0:T(2,128)}, u32[]{:S(2)}) copy-start(f32[128,2,128]{2,1,0:T(2,128)} %param.11) | copy-start | bytes 393220
  36.3 67.4 %all-to-all-start = ((bf16[32,128,2,128]{1,3,2,0:T(8,128)(2,1)}), bf16[32,128,2,128]{1,3,2,0:T(8,128)(2,1)S(1)}, u32[]{:S(2)}, u32[]{:S(2)}) async-start(bf16[32,128,2,128]{1,3,2,0:T(8,128)(2,1)} %bitcast.40), calls=%async_computation | async-start | bytes 4194304 | tf_op jit(solution)/shard_map/all_to_all | solution.py:34
  50.8 53.2 %collective-permute-start = (f32[128,2,1]{0,2,1:T(1,128)S(1)}, f32[128,2,1]{0,2,1:T(1,128)S(1)}, u32[]{:S(2)}, u32[]{:S(2)}) collective-permute-start(f32[128,2,1]{0,2,1:T(1,128)S(1)} %get-tuple-element.20), channel_id=1, source_target_pairs={{0,1},{1,2},{2,3},{3,4},{4,5},{5,6},{6,7},{8,9},{9,10},{10,11},{11... | collective-permute-start | bytes 3080 | tf_op jit(solution)/shard_map/ppermute | solution.py:17
  52.1 51.9 %collective-permute-start.1 = (f32[128,2,1]{0,2,1:T(1,128)S(1)}, f32[128,2,1]{0,2,1:T(1,128)S(1)}, u32[]{:S(2)}, u32[]{:S(2)}) collective-permute-start(f32[128,2,1]{0,2,1:T(1,128)S(1)} %get-tuple-element.21), channel_id=1, source_target_pairs={{1,0},{2,1},{3,2},{4,3},{5,4},{6,5},{7,6},{9,8},{10,9},{11,10},{12... | collective-permute-start | bytes 3080 | tf_op jit(solution)/shard_map/ppermute | solution.py:19
  106.0 58.0 %all-to-all-start.1 = ((bf16[32,128,2,128]{1,3,2,0:T(8,128)(2,1)}), bf16[32,128,2,128]{1,3,2,0:T(8,128)(2,1)S(1)}, u32[]{:S(2)}, u32[]{:S(2)}) async-start(bf16[32,128,2,128]{1,3,2,0:T(8,128)(2,1)} %broadcast_in_dim.35), calls=%async_computation.1 | async-start | bytes 4194304 | tf_op jit(solution)/shard_map/all_to_all | solution.py:46
where the time goes:
time: 233 us
  waiting for transfers between devices  102 us (44%)
  matrix products  89.4 us (38%)
  starting transfers between devices  22.1 us (9%)
  local copies, waits for them, and re-layouts  13.1 us (6%)
  other arithmetic  4.8 us (2%)
    all_to_all x1, waiting for transfers between devices, from_everyone(): return lax.all_to_all(copies, axis, split_axis=0, concat_axis=0, tiled=True)  52.1 us
    all_to_all x1, waiting for transfers between devices, sent_and_summed(): lax.all_to_all(parts, axis, split_axis=0, concat_axis=0, tiled=True)  50.3 us
    dot_general x1, matrix products, shards(): jnp.einsum('ajk,ajrq->akrq', onehot, images, precision=lax.Precision.HIGH...  40.2 us
    dot_general x1, matrix products, shards(): jnp.einsum('ajrq,ajqp->jpr', windows, tile_part, preferred_element_type=j...  21.2 us
    dot_general x1, matrix products, shards(): jnp.einsum('jpr,ajqp->ajrq', piece.reshape(tile_count, block_size, row_co...  19 us
    all_to_all x1, starting transfers between devices, sent_and_summed(): lax.all_to_all(parts, axis, split_axis=0, concat_axis=0, tiled=True)  14.4 us
    dot_general x1, matrix products, shards(): jnp.einsum('ajk,akrq->ajrq', onehot, stacked, preferred_element_type=jnp....  9.12 us
    slice x1, local copies, waits for them, and re-layouts, shards(): grouped[:, offset_index]  7.57 us
  transfers between devices with their start and end apart: 4, of which 2 were waited for; matrix products, arithmetic and copies ran while one was open for 1% of the time, Pallas kernels for 0%

commit v1 on v0

v1 whole, which is shorter than its diff:
```python
import functools

import jax
import jax.numpy as jnp
from jax import lax
from jax.experimental import pallas as pl
from jax.experimental.pallas import tpu as pltpu
from jax.sharding import PartitionSpec as P

SMOOTHING = 0.25
MESH = pl.DeviceIdType.MESH
BF = jnp.bfloat16
F32 = jnp.float32
NX, NY, NH = 4, 4, 2
SLABS = 8
GROUP_ORDER = (2, 1, 3, 0)


def device(x, y, h, s):
    return (y * (NH * NX) + h * NX + x, s)


def wrapped(v, n):
    return lax.rem(v + n, n)


def exchange_kernel(
    band_ref,
    id_ref,
    weight_ref,
    upd_hbm,
    tiles_hbm,
    vol_ref,
    vnext_ref,
    gath,
    upd,
    tiles,
    scaled,
    part,
    vt,
    halo,
    smooth,
    smooth_in,
    r1,
    s2,
    r2,
    keep,
    zs,
    rz,
    upd_sem,
    tile_sem,
    halo_ss,
    halo_rs,
    sm_ss,
    sm_rs,
    ss1,
    rs1,
    ss2,
    rs2,
    zss,
    zrs,
    ass1,
    ars1,
    ass2,
    ars2,
):
    me = lax.axis_index("ang")
    s = lax.axis_index("slab")
    x = lax.rem(me, NX)
    h = lax.rem(me // NX, NH)
    y = me // (NX * NH)
    sl = wrapped(s - 1, SLABS)
    sr = wrapped(s + 1, SLABS)
    xs = [wrapped(x + d, NX) for d in range(4)]
    ys = [wrapped(y + d, NY) for d in range(4)]

    barrier = pltpu.get_barrier_semaphore()
    peers = (
        [device(xs[d], y, h, s) for d in (1, 2, 3)]
        + [device(x, ys[d], h, s) for d in (1, 2, 3)]
        + [device(x, y, 1 - h, s), device(x, y, h, sl), device(x, y, h, sr)]
    )
    for peer in peers:
        pl.semaphore_signal(barrier, inc=1, device_id=peer, device_id_type=MESH)

    upd_copies = [pltpu.make_async_copy(upd_hbm.at[a], upd.at[a], upd_sem.at[a]) for a in range(4)]
    for copy in upd_copies:
        copy.start()

    def tile_copy(ty, th, tx):
        j = ty * (NH * NX) + th * NX + tx
        return pltpu.make_async_copy(tiles_hbm.at[:, j], tiles.at[j], tile_sem.at[j])

    for d in GROUP_ORDER:

        def start_tiles(i, carry, d=d):
            tile_copy(i, 0, xs[d]).start()
            tile_copy(ys[d], 1, i).start()
            return carry

        lax.fori_loop(0, 4, start_tiles, 0)

    for c in range(2):
        vt[c] = vol_ref[:, c, :].T
    lanes = lax.broadcasted_iota(jnp.int32, (1, 128), 1)
    for a in range(4):
        matched = jnp.where(lanes == id_ref[a], weight_ref[...], 0.0)
        chosen = jnp.sum(matched, axis=1, keepdims=True)
        upd_copies[a].wait()
        value = (chosen * upd[a]).astype(BF)
        for k in range(3):
            scaled[3 * a + k] = value[:, 128 * k : 128 * k + 256]

    def one_tile(ty, th, tx):
        j = ty * (NH * NX) + th * NX + tx
        tile_copy(ty, th, tx).wait()
        windows = [scaled[3 * a + band_ref[a, j]] for a in range(4)]
        total = jnp.dot(
            jnp.concatenate(windows, axis=1),
            tiles[j].reshape(4 * 256, 128),
            preferred_element_type=F32,
        )
        part[ty, th, tx] = total.astype(BF)

    def remote(src, dst, send, recv, where):
        return pltpu.make_async_remote_copy(
            src_ref=src,
            dst_ref=dst,
            send_sem=send,
            recv_sem=recv,
            device_id=where,
            device_id_type=MESH,
        )

    def rows(c):
        return slice(c * 128, c * 128 + 128)

    def first(path, c, d):
        if path == 0:
            src, where = part.at[:, 0, xs[d], rows(c), :], device(xs[d], y, h, s)
        else:
            src, where = part.at[ys[d], 1, :, rows(c), :], device(x, ys[d], h, s)
        return remote(
            src, r1.at[path, c, d - 1], ss1.at[path, c, d - 1], rs1.at[path, c, d - 1], where
        )

    def second(path, c, d):
        where = device(x, ys[d], h, s) if path == 0 else device(xs[d], y, h, s)
        return remote(
            s2.at[path, c, d - 1],
            r2.at[path, c, d - 1],
            ss2.at[path, c, d - 1],
            rs2.at[path, c, d - 1],
            where,
        )

    def across(path, c):
        return remote(
            zs.at[path, c], rz.at[path, c], zss.at[path, c], zrs.at[path, c], device(x, y, 1 - h, s)
        )

    def gather1(path, c, d):
        where = device(x, ys[d], h, s) if path == 0 else device(xs[d], y, h, s)
        ref = gath.at[y, path, x, :, rows(c)]
        return remote(ref, ref, ass1.at[path, c, d - 1], ars1.at[path, c, d - 1], where)

    def gather2(path, c, d):
        if path == 0:
            ref, where = gath.at[:, 0, x, :, rows(c)], device(xs[d], y, h, s)
        else:
            ref, where = gath.at[y, 1, :, :, rows(c)], device(x, ys[d], h, s)
        return remote(ref, ref, ass2.at[path, c, d - 1], ars2.at[path, c, d - 1], where)

    def halo_copy(c, side):
        if side == 0:
            src, where = vt.at[c, 120:128, :], device(x, y, h, sr)
        else:
            src, where = vt.at[c, 0:8, :], device(x, y, h, sl)
        return remote(src, halo.at[c, side], halo_ss.at[c, side], halo_rs.at[c, side], where)

    smooth_copy = remote(smooth, smooth_in, sm_ss, sm_rs, device(x, y, 1 - h, s))

    for position, d in enumerate(GROUP_ORDER):

        def group(i, carry, d=d):
            for u in range(2):
                one_tile(2 * i + u, 0, xs[d])
                one_tile(ys[d], 1, 2 * i + u)
            return carry

        lax.fori_loop(0, 2, group, 0)
        if position == 0:
            pl.semaphore_wait(barrier, len(peers))
            for c in range(2):
                halo_copy(c, 0).start()
                halo_copy(c, 1).start()
        if d:
            for c in range(2):
                first(0, c, d).start()
                first(1, c, d).start()
        if position == 1:
            for c in range(2):
                halo_copy(c, 0).wait_recv()
                halo_copy(c, 1).wait_recv()
                mid = vt[c]
                row = lax.broadcasted_iota(jnp.int32, (128, 128), 0)
                low = jnp.where(s > 0, halo[c, 0, 7:8, :], 0.0)
                high = jnp.where(s < SLABS - 1, halo[c, 1, 0:1, :], 0.0)
                before = jnp.where(row == 0, low, pltpu.roll(mid, 1, 0))
                after = jnp.where(row == 127, high, pltpu.roll(mid, 127, 0))
                smooth[c] = mid - SMOOTHING * (2.0 * mid - before - after)
            smooth_copy.start()

    for c in range(2):
        for path in range(2):
            for d in (1, 2, 3):
                first(path, c, d).wait_recv()
            for d in (2, 1, 3, 0):
                at = ys[d] if path == 0 else xs[d]
                own = part[at, 0, x, rows(c), :] if path == 0 else part[y, 1, at, rows(c), :]
                total = own.astype(F32)
                for k in range(3):
                    total = total + r1[path, c, k, at].astype(F32)
                if d:
                    s2[path, c, d - 1] = total.astype(BF)
                    second(path, c, d).start()
                else:
                    keep[path, c] = total

    for c in range(2):
        for path in range(2):
            for d in (1, 2, 3):
                second(path, c, d).wait_recv()
            total = keep[path, c]
            for k in range(3):
                total = total + r2[path, c, k].astype(F32)
            keep[path, c] = total
            zs[path, c] = total.astype(BF)
            across(path, c).start()

    smooth_copy.wait_recv()
    for c in range(2):
        fields = []
        for path in range(2):
            across(path, c).wait_recv()
            base = jnp.where(h == path, smooth[c], smooth_in[c])
            field = base + (keep[path, c] + rz[path, c].astype(F32))
            if c == 1:
                field = jnp.maximum(field, 0.0)
            field = field.T
            fields.append(field)
            gath[y, path, x, :, rows(c)] = field.astype(BF)
            for d in (2, 1, 3):
                gather1(path, c, d).start()
        vnext_ref[:, c, :] = jnp.where(h == 0, fields[0], fields[1])

    for c in range(2):
        for path in range(2):
            for d in (1, 2, 3):
                gather1(path, c, d).wait_recv()
            for d in (2, 1, 3):
                gather2(path, c, d).start()

    for c in range(2):
        for path in range(2):
            for d in (1, 2, 3):
                gather2(path, c, d).wait_recv()

    smooth_copy.wait_send()
    for c in range(2):
        halo_copy(c, 0).wait_send()
        halo_copy(c, 1).wait_send()
        for path in range(2):
            across(path, c).wait_send()
            for d in (1, 2, 3):
                first(path, c, d).wait_send()
                second(path, c, d).wait_send()
                gather1(path, c, d).wait_send()
                gather2(path, c, d).wait_send()


def placed_rows(tile, start):
    low, high = tile[:128], tile[128:]
    zero = jnp.zeros_like(low)
    return jnp.concatenate(
        [
            jnp.where(start == 0, low, zero),
            jnp.where(start == 0, high, jnp.where(start == 1, low, zero)),
            jnp.where(start == 1, high, jnp.where(start == 2, low, zero)),
            jnp.where(start == 2, high, zero),
        ],
        axis=0,
    )


def project_kernel(band_ref, tiles_ref, gath_ref, out_ref, acc):
    a = pl.program_id(0)

    def group(g, carry):
        left = jnp.concatenate(
            [placed_rows(tiles_ref[0, g * 8 + u], band_ref[a, g * 8 + u]) for u in range(8)], axis=1
        )
        right = gath_ref[pl.ds(g * 8, 8)].reshape(8 * 128, 256)
        term = jnp.dot(left, right, preferred_element_type=F32)
        acc[...] = jnp.where(g == 0, term, acc[...] + term)
        return carry

    lax.fori_loop(0, 4, group, 0)
    out_ref[0] = acc[...].T


def shards(updates, interp_tiles, band_start, angle_id, angle_weight, volume):
    smem = pl.BlockSpec(memory_space=pltpu.SMEM)
    vmem = pl.BlockSpec(memory_space=pltpu.VMEM)
    hbm = pl.BlockSpec(memory_space=pl.ANY)
    dma = pltpu.SemaphoreType.DMA
    vnext, gath = pl.pallas_call(
        exchange_kernel,
        out_shape=(
            jax.ShapeDtypeStruct((128, 2, 128), F32),
            jax.ShapeDtypeStruct((4, 2, 4, 128, 256), BF),
        ),
        in_specs=[smem, smem, vmem, hbm, hbm, vmem],
        out_specs=(vmem, vmem),
        scratch_shapes=[
            pltpu.VMEM((4, 256, 512), F32),
            pltpu.VMEM((32, 4, 256, 128), BF),
            pltpu.VMEM((12, 256, 256), BF),
            pltpu.VMEM((4, 2, 4, 256, 128), BF),
            pltpu.VMEM((2, 128, 128), F32),
            pltpu.VMEM((2, 2, 8, 128), F32),
            pltpu.VMEM((2, 128, 128), F32),
            pltpu.VMEM((2, 128, 128), F32),
            pltpu.VMEM((2, 2, 3, 4, 128, 128), BF),
            pltpu.VMEM((2, 2, 3, 128, 128), BF),
            pltpu.VMEM((2, 2, 3, 128, 128), BF),
            pltpu.VMEM((2, 2, 128, 128), F32),
            pltpu.VMEM((2, 2, 128, 128), BF),
            pltpu.VMEM((2, 2, 128, 128), BF),
            dma((4,)),
            dma((32,)),
            dma((2, 2)),
            dma((2, 2)),
            dma,
            dma,
            dma((2, 2, 3)),
            dma((2, 2, 3)),
            dma((2, 2, 3)),
            dma((2, 2, 3)),
            dma((2, 2)),
            dma((2, 2)),
            dma((2, 2, 3)),
            dma((2, 2, 3)),
            dma((2, 2, 3)),
            dma((2, 2, 3)),
        ],
        compiler_params=pltpu.CompilerParams(
            collective_id=0, has_side_effects=True, vmem_limit_bytes=44 * 2**20
        ),
        name="exchange",
    )(
        band_start,
        angle_id,
        angle_weight.reshape(1, 128),
        updates.reshape(4, 256, 512),
        interp_tiles,
        volume,
    )
    projection = pl.pallas_call(
        project_kernel,
        grid=(4,),
        out_shape=jax.ShapeDtypeStruct((4, 256, 512), F32),
        in_specs=[
            smem,
            pl.BlockSpec((1, 32, 256, 128), lambda a: (a, 0, 0, 0)),
            vmem,
        ],
        out_specs=pl.BlockSpec((1, 256, 512), lambda a: (a, 0, 0)),
        scratch_shapes=[pltpu.VMEM((512, 256), F32)],
        compiler_params=pltpu.CompilerParams(vmem_limit_bytes=32 * 2**20),
        name="project",
    )(band_start, interp_tiles, gath.reshape(32, 128, 256))
    return vnext, projection.reshape(4, 2, 128, 512)


def solution(mesh):
    placed = (
        P("ang", None, "slab", None),
        P("ang", None, None, None),
        P("ang", None),
        P("ang"),
        P(),
        P("ang", None, "slab"),
    )
    return jax.shard_map(
        shards,
        mesh=mesh,
        in_specs=placed,
        out_specs=(P("ang", None, "slab"), P("ang", None, "slab", None)),
        check_vma=False,
    )
```

time: 233 us -> 68.1 us (0.29)
  the two profiles are of different devices: /device:TPU:2 before, /device:TPU:1 now
where the time goes in v1:
time: 68.1 us; the launch traced here: 67.9 us
  Pallas kernels  62.1 us (91%)
  local copies, waits for them, and re-layouts  5.14 us (8%)
    pallas_call x1, Pallas kernels, shards(): pl.pallas_call(exchange_kernel, out_shape=(jax.ShapeDtypeStruct((128, 2,...  52.6 us
    pallas_call x1, Pallas kernels, shards(): pl.pallas_call(project_kernel, grid=(4,), out_shape=jax.ShapeDtypeStruct(...  9.48 us
    unnamed x13, local copies, waits for them, and re-layouts  5.14 us

profile of v1, /device:TPU:1, one launch (start us, length us, event | category | flops | bytes accessed | tf_op | source)
XLA Modules:
  0.0 67.9 jit_solution(10004801798694155333)
XLA Ops:
  0.6 0.0 copy-start.1
  0.6 1.6 %copy-done.1 = f32[4,2,128,512]{3,2,1,0:T(8,128)S(1)} copy-done((f32[4,2,128,512]{3,2,1,0:T(8,128)S(1)}, f32[4,2,128,512]{3,2,1,0:T(8,128)}, u32[]{:S(2)}) %copy-start.1) | copy-done | bytes 2097176
  2.2 0.0 copy-start.2
  2.2 0.9 %copy-done.2 = f32[128,2,128]{2,1,0:T(2,128)S(1)} copy-done((f32[128,2,128]{2,1,0:T(2,128)S(1)}, f32[128,2,128]{2,1,0:T(2,128)}, u32[]{:S(2)}) %copy-start.2) | copy-done | bytes 131096
  3.1 0.0 copy-start.3
  3.1 0.7 %copy-done.3 = s32[4,32]{1,0:T(4,128)S(1)} copy-done((s32[4,32]{1,0:T(4,128)S(1)}, s32[4,32]{1,0:T(4,128)}, u32[]{:S(2)}) %copy-start.3) | copy-done | bytes 536
  3.8 0.0 copy-start.4
  3.8 0.7 copy-done.4
  4.5 0.0 copy-start.5
  4.5 0.7 copy-done.5
  5.1 0.0 copy-start
  5.1 52.6 %exchange.1 = (f32[128,2,128]{2,1,0:T(2,128)S(1)}, bf16[4,2,4,128,256]{4,3,2,1,0:T(8,128)(2,1)S(1)}) custom-call(s32[4,32]{1,0:T(4,128)S(1)} %copy-done.3, s32[4]{0:T(128)S(1)} %copy-done.4, f32[1,128]{1,0:T(1,128)S(1)} %bitcast.6, f32[4,256,512]{2,1,0:T(8,128)S(1)} %bitcast.4, bf16[4,32,256,128]{3,2,1,0:T(8,128)(2,1)} %tiles_ref.1, f32[128,2,128]{2,1,0:T(2,128)S(1)} %copy-done.2), custom_call_target="tpu_custom_call" | custom-call | tf_op jit(solution)/shard_map/exchange/pallas_call | solution.py:317
  57.8 0.0 copy-done
  57.8 9.5 %project.1 = f32[4,256,512]{2,1,0:T(8,128)} custom-call(s32[4,32]{1,0:T(4,128)S(1)} %copy-done.3, bf16[4,32,256,128]{3,2,1,0:T(8,128)(2,1)S(1)} %copy-done, bf16[32,128,256]{2,1,0:T(8,128)(2,1)S(1)} %bitcast.5), custom_call_target="tpu_custom_call" | custom-call | tf_op jit(solution)/shard_map/project/pallas_call | solution.py:369
  67.2 0.7 copy.9
Async XLA Ops:
  0.6 1.6 %copy-start.1 = (f32[4,2,128,512]{3,2,1,0:T(8,128)S(1)}, f32[4,2,128,512]{3,2,1,0:T(8,128)}, u32[]{:S(2)}) copy-start(f32[4,2,128,512]{3,2,1,0:T(8,128)} %param.6) | copy-start | bytes 6291460
  2.2 0.9 %copy-start.2 = (f32[128,2,128]{2,1,0:T(2,128)S(1)}, f32[128,2,128]{2,1,0:T(2,128)}, u32[]{:S(2)}) copy-start(f32[128,2,128]{2,1,0:T(2,128)} %vol_ref.1) | copy-start | bytes 393220
  3.1 0.7 %copy-start.3 = (s32[4,32]{1,0:T(4,128)S(1)}, s32[4,32]{1,0:T(4,128)}, u32[]{:S(2)}) copy-start(s32[4,32]{1,0:T(4,128)} %band_ref.3) | copy-start | bytes 1540
  3.8 0.7 copy-start.4
  4.5 0.7 copy-start.5
  5.1 52.6 %copy-start = (bf16[4,32,256,128]{3,2,1,0:T(8,128)(2,1)S(1)}, bf16[4,32,256,128]{3,2,1,0:T(8,128)(2,1)}, u32[]{:S(2)}) copy-start(bf16[4,32,256,128]{3,2,1,0:T(8,128)(2,1)} %tiles_ref.1) | copy-start | bytes 25165828

commit v2 on v1

v2 whole, which is shorter than its diff:
```python
import jax
import jax.numpy as jnp
from jax import lax
from jax.experimental import pallas as pl
from jax.experimental.pallas import tpu as pltpu
from jax.sharding import PartitionSpec as P

SMOOTHING = 0.25
MESH = pl.DeviceIdType.MESH
BF = jnp.bfloat16
F32 = jnp.float32
NX, NY, NH = 4, 4, 2
SLABS = 8
ANG = 4
FAR = (2, 1, 3)


def device(x, y, h, s):
    return (y * (NH * NX) + h * NX + x, s)


def wrapped(v, n):
    return lax.rem(v + n, n)


def placed_rows(tile, start):
    low, high = tile[:128], tile[128:]
    zero = jnp.zeros_like(low)
    return jnp.concatenate(
        [
            jnp.where(start == 0, low, zero),
            jnp.where(start == 0, high, jnp.where(start == 1, low, zero)),
            jnp.where(start == 1, high, jnp.where(start == 2, low, zero)),
            jnp.where(start == 2, high, zero),
        ],
        axis=0,
    )


def whole_kernel(
    band_hbm,
    id_hbm,
    weight_hbm,
    upd_hbm,
    tiles_hbm,
    vol_hbm,
    vnext_ref,
    out_ref,
    band_ref,
    id_ref,
    weight_ref,
    vol_ref,
    upd,
    tiles,
    scaled,
    part,
    vt,
    halo,
    smooth,
    smooth_in,
    r1,
    s2,
    r2,
    keep,
    zs,
    rz,
    gath,
    acc,
    in_sem,
    tile_sem,
    halo_ss,
    halo_rs,
    sm_ss,
    sm_rs,
    ss1,
    rs1,
    ss2,
    rs2,
    zss,
    zrs,
    ass1,
    ars1,
    ass2,
    ars2,
):
    me = lax.axis_index("ang")
    s = lax.axis_index("slab")
    x = lax.rem(me, NX)
    h = lax.rem(me // NX, NH)
    y = me // (NX * NH)
    sl = wrapped(s - 1, SLABS)
    sr = wrapped(s + 1, SLABS)
    xs = [wrapped(x + d, NX) for d in range(4)]
    ys = [wrapped(y + d, NY) for d in range(4)]

    barrier = pltpu.get_barrier_semaphore()
    peers = (
        [device(xs[d], y, h, s) for d in (1, 2, 3)]
        + [device(x, ys[d], h, s) for d in (1, 2, 3)]
        + [device(x, y, 1 - h, s), device(x, y, h, sl), device(x, y, h, sr)]
    )
    for peer in peers:
        pl.semaphore_signal(barrier, inc=1, device_id=peer, device_id_type=MESH)

    def tile_copy(ty, th, tx):
        j = ty * (NH * NX) + th * NX + tx
        return pltpu.make_async_copy(tiles_hbm.at[:, j], tiles.at[j], tile_sem.at[j])

    def start_tiles(d):
        def body(i, carry):
            tile_copy(i, 0, xs[d]).start()
            tile_copy(ys[d], 1, i).start()
            return carry

        lax.fori_loop(0, 4, body, 0)

    band_copy = pltpu.make_async_copy(band_hbm, band_ref, in_sem.at[0])
    id_copy = pltpu.make_async_copy(id_hbm, id_ref, in_sem.at[1])
    weight_copy = pltpu.make_async_copy(weight_hbm, weight_ref, in_sem.at[2])
    vol_copy = pltpu.make_async_copy(vol_hbm, vol_ref, in_sem.at[3])
    upd_copies = [pltpu.make_async_copy(upd_hbm.at[:, c], upd.at[c], in_sem.at[4 + c]) for c in (0, 1)]
    id_copy.start()
    weight_copy.start()
    upd_copies[0].start()
    band_copy.start()
    start_tiles(2)
    vol_copy.start()
    start_tiles(1)
    start_tiles(3)
    upd_copies[1].start()
    start_tiles(0)

    def rows(c):
        return slice(c * 128, c * 128 + 128)

    lanes = lax.broadcasted_iota(jnp.int32, (1, 128), 1)
    id_copy.wait()
    weight_copy.wait()
    chosen = [
        jnp.sum(jnp.where(lanes == id_ref[a], weight_ref[...], 0.0), axis=1, keepdims=True)
        for a in range(ANG)
    ]

    def scale(c):
        upd_copies[c].wait()
        for a in range(ANG):
            value = (chosen[a] * upd[c, a]).astype(BF)
            for k in range(3):
                scaled[c, 3 * a + k] = value[:, 128 * k : 128 * k + 256]

    def one_tile(c, ty, th, tx):
        j = ty * (NH * NX) + th * NX + tx
        if c == 0:
            tile_copy(ty, th, tx).wait()
        windows = [scaled[c, 3 * a + band_ref[a, j]] for a in range(ANG)]
        total = jnp.dot(
            jnp.concatenate(windows, axis=1),
            tiles[j].reshape(ANG * 256, 128),
            preferred_element_type=F32,
        )
        part[ty, th, tx, rows(c), :] = total.astype(BF)

    def back(c, d):
        def body(i, carry):
            for u in range(2):
                one_tile(c, 2 * i + u, 0, xs[d])
                one_tile(c, ys[d], 1, 2 * i + u)
            return carry

        lax.fori_loop(0, 2, body, 0)

    def remote(src, dst, send, recv, where):
        return pltpu.make_async_remote_copy(
            src_ref=src,
            dst_ref=dst,
            send_sem=send,
            recv_sem=recv,
            device_id=where,
            device_id_type=MESH,
        )

    def first(path, c, d):
        if path == 0:
            src, where = part.at[:, 0, xs[d], rows(c), :], device(xs[d], y, h, s)
        else:
            src, where = part.at[ys[d], 1, :, rows(c), :], device(x, ys[d], h, s)
        return remote(
            src, r1.at[path, c, d - 1], ss1.at[path, c, d - 1], rs1.at[path, c, d - 1], where
        )

    def inner(path, d):
        return device(x, ys[d], h, s) if path == 0 else device(xs[d], y, h, s)

    def outer(path, d):
        return device(xs[d], y, h, s) if path == 0 else device(x, ys[d], h, s)

    def second(path, c, d):
        return remote(
            s2.at[path, c, d - 1],
            r2.at[path, c, d - 1],
            ss2.at[path, c, d - 1],
            rs2.at[path, c, d - 1],
            inner(path, d),
        )

    def across(path, c):
        return remote(
            zs.at[path, c], rz.at[path, c], zss.at[path, c], zrs.at[path, c], device(x, y, 1 - h, s)
        )

    def slot(path, c, k):
        if path == 0:
            return gath.at[ys[(4 - k) % 4], 0, x, :, rows(c)]
        return gath.at[y, 1, xs[(4 - k) % 4], :, rows(c)]

    def gather1(path, c, d):
        ref = slot(path, c, 0)
        return remote(ref, ref, ass1.at[path, c, d - 1], ars1.at[path, c, d - 1], inner(path, d))

    def gather2(path, c, d, k):
        ref = slot(path, c, k)
        return remote(
            ref, ref, ass2.at[path, c, d - 1, k], ars2.at[path, c, d - 1, k], outer(path, d)
        )

    def halo_copy(c, side):
        if side == 0:
            src, where = vt.at[c, 120:128, :], device(x, y, h, sr)
        else:
            src, where = vt.at[c, 0:8, :], device(x, y, h, sl)
        return remote(src, halo.at[c, side], halo_ss.at[c, side], halo_rs.at[c, side], where)

    smooth_copy = remote(smooth, smooth_in, sm_ss, sm_rs, device(x, y, 1 - h, s))

    def send_first(c, d):
        first(0, c, d).start()
        first(1, c, d).start()

    def sum_first(c):
        for path in range(2):
            for d in (1, 2, 3):
                first(path, c, d).wait_recv()
            for d in FAR + (0,):
                at = ys[d] if path == 0 else xs[d]
                own = part[at, 0, x, rows(c), :] if path == 0 else part[y, 1, at, rows(c), :]
                total = own.astype(F32)
                for k in range(3):
                    total = total + r1[path, c, k, at].astype(F32)
                if d:
                    s2[path, c, d - 1] = total.astype(BF)
                    second(path, c, d).start()
                else:
                    keep[path, c] = total

    def sum_second(c):
        for path in range(2):
            for d in (1, 2, 3):
                second(path, c, d).wait_recv()
            total = keep[path, c]
            for k in range(3):
                total = total + r2[path, c, k].astype(F32)
            keep[path, c] = total
            zs[path, c] = total.astype(BF)
            across(path, c).start()

    def finish_volume(c):
        fields = []
        for path in range(2):
            across(path, c).wait_recv()
            base = jnp.where(h == path, smooth[c], smooth_in[c])
            field = base + (keep[path, c] + rz[path, c].astype(F32))
            if c == 1:
                field = jnp.maximum(field, 0.0)
            field = field.T
            fields.append(field)
            gath[y, path, x, :, rows(c)] = field.astype(BF)
            for d in FAR:
                gather1(path, c, d).start()
            for d in FAR:
                gather2(path, c, d, 0).start()
        vnext_ref[:, c, :] = jnp.where(h == 0, fields[0], fields[1])

    def relay(c):
        for k in (1, 3, 2):
            for path in range(2):
                gather1(path, c, k).wait_recv()
                for d in FAR:
                    gather2(path, c, d, k).start()

    def project(c, d, begin, end):
        tx, ty = xs[(4 - d) % 4], ys[(4 - d) % 4]
        if d:
            for path in range(2):
                for k in range(4):
                    gather2(path, c, d, k).wait_recv()
        right = jnp.concatenate(
            [gath[i, 0, tx, :, rows(c)] for i in range(4)]
            + [gath[ty, 1, i, :, rows(c)] for i in range(4)],
            axis=0,
        )
        picks = [i * 8 + tx for i in range(4)] + [ty * 8 + 4 + i for i in range(4)]

        def body(g, carry):
            for u in range(2):
                a = 2 * g + u
                left = jnp.concatenate(
                    [placed_rows(tiles[j, a], band_ref[a, j]) for j in picks], axis=1
                )
                term = jnp.dot(left, right, preferred_element_type=F32)
                if not begin:
                    term = term + acc[c, a]
                if end:
                    out_ref[a, rows(c), :] = term.T
                else:
                    acc[c, a] = term
            return carry

        lax.fori_loop(0, 2, body, 0)

    scale(0)
    band_copy.wait()
    back(0, 2)
    vol_copy.wait()
    for c in range(2):
        vt[c] = vol_ref[:, c, :].T
    pl.semaphore_wait(barrier, len(peers))
    for c in range(2):
        halo_copy(c, 0).start()
        halo_copy(c, 1).start()
    send_first(0, 2)
    back(0, 1)
    send_first(0, 1)
    back(0, 3)
    send_first(0, 3)
    back(0, 0)
    scale(1)
    back(1, 2)
    send_first(1, 2)
    for c in range(2):
        halo_copy(c, 0).wait_recv()
        halo_copy(c, 1).wait_recv()
        mid = vt[c]
        row = lax.broadcasted_iota(jnp.int32, (128, 128), 0)
        low = jnp.where(s > 0, halo[c, 0, 7:8, :], 0.0)
        high = jnp.where(s < SLABS - 1, halo[c, 1, 0:1, :], 0.0)
        before = jnp.where(row == 0, low, pltpu.roll(mid, 1, 0))
        after = jnp.where(row == 127, high, pltpu.roll(mid, 127, 0))
        smooth[c] = mid - SMOOTHING * (2.0 * mid - before - after)
    smooth_copy.start()
    back(1, 1)
    send_first(1, 1)
    back(1, 3)
    sum_first(0)
    send_first(1, 3)
    back(1, 0)
    sum_second(0)
    sum_first(1)
    smooth_copy.wait_recv()
    finish_volume(0)
    sum_second(1)
    relay(0)
    project(0, 0, True, False)
    finish_volume(1)
    relay(1)
    project(0, 1, False, False)
    project(0, 3, False, False)
    project(0, 2, False, True)
    project(1, 0, True, False)
    project(1, 1, False, False)
    project(1, 3, False, False)
    project(1, 2, False, True)

    smooth_copy.wait_send()
    for c in range(2):
        halo_copy(c, 0).wait_send()
        halo_copy(c, 1).wait_send()
        for path in range(2):
            across(path, c).wait_send()
            for d in (1, 2, 3):
                first(path, c, d).wait_send()
                second(path, c, d).wait_send()
                gather1(path, c, d).wait_send()
                for k in range(4):
                    gather2(path, c, d, k).wait_send()


def shards(updates, interp_tiles, band_start, angle_id, angle_weight, volume):
    vmem = pl.BlockSpec(memory_space=pltpu.VMEM)
    hbm = pl.BlockSpec(memory_space=pl.ANY)
    dma = pltpu.SemaphoreType.DMA
    vnext, projection = pl.pallas_call(
        whole_kernel,
        out_shape=(
            jax.ShapeDtypeStruct((128, 2, 128), F32),
            jax.ShapeDtypeStruct((4, 256, 512), F32),
        ),
        in_specs=[hbm] * 6,
        out_specs=(vmem, vmem),
        scratch_shapes=[
            pltpu.SMEM((4, 32), jnp.int32),
            pltpu.SMEM((4,), jnp.int32),
            pltpu.VMEM((1, 128), F32),
            pltpu.VMEM((128, 2, 128), F32),
            pltpu.VMEM((2, 4, 128, 512), F32),
            pltpu.VMEM((32, 4, 256, 128), BF),
            pltpu.VMEM((2, 12, 128, 256), BF),
            pltpu.VMEM((4, 2, 4, 256, 128), BF),
            pltpu.VMEM((2, 128, 128), F32),
            pltpu.VMEM((2, 2, 8, 128), F32),
            pltpu.VMEM((2, 128, 128), F32),
            pltpu.VMEM((2, 128, 128), F32),
            pltpu.VMEM((2, 2, 3, 4, 128, 128), BF),
            pltpu.VMEM((2, 2, 3, 128, 128), BF),
            pltpu.VMEM((2, 2, 3, 128, 128), BF),
            pltpu.VMEM((2, 2, 128, 128), F32),
            pltpu.VMEM((2, 2, 128, 128), BF),
            pltpu.VMEM((2, 2, 128, 128), BF),
            pltpu.VMEM((4, 2, 4, 128, 256), BF),
            pltpu.VMEM((2, 4, 512, 128), F32),
            dma((6,)),
            dma((32,)),
            dma((2, 2)),
            dma((2, 2)),
            dma,
            dma,
            dma((2, 2, 3)),
            dma((2, 2, 3)),
            dma((2, 2, 3)),
            dma((2, 2, 3)),
            dma((2, 2)),
            dma((2, 2)),
            dma((2, 2, 3)),
            dma((2, 2, 3)),
            dma((2, 2, 3, 4)),
            dma((2, 2, 3, 4)),
        ],
        compiler_params=pltpu.CompilerParams(
            collective_id=0, has_side_effects=True, vmem_limit_bytes=63 * 2**20
        ),
        name="exchange",
    )(band_start, angle_id, angle_weight.reshape(1, 128), updates, interp_tiles, volume)
    return vnext, projection.reshape(4, 2, 128, 512)


def solution(mesh):
    placed = (
        P("ang", None, "slab", None),
        P("ang", None, None, None),
        P("ang", None),
        P("ang"),
        P(),
        P("ang", None, "slab"),
    )
    return jax.shard_map(
        shards,
        mesh=mesh,
        in_specs=placed,
        out_specs=(P("ang", None, "slab"), P("ang", None, "slab", None)),
        check_vma=False,
    )
```

time: 68.1 us -> 63.3 us (0.930)
  the two profiles are of different devices: /device:TPU:1 before, /device:TPU:2 now
where the time goes in v2:
time: 63.3 us; the launch traced here: 62.8 us
  Pallas kernels  57.5 us (91%)
  local copies, waits for them, and re-layouts  4.65 us (7%)
  between operations  0.64 us (1%)
    pallas_call x1, Pallas kernels, shards(): pl.pallas_call(whole_kernel, out_shape=(jax.ShapeDtypeStruct((128, 2, 128...  57.5 us
    unnamed x2, local copies, waits for them, and re-layouts  4.65 us

profile of v2, /device:TPU:2, one launch (start us, length us, event | category | flops | bytes accessed | tf_op | source)
XLA Modules:
  0.0 62.8 jit_solution(3122664413469081608)
XLA Ops:
  0.6 57.5 %exchange.1 = (f32[128,2,128]{2,1,0:T(2,128)}, f32[4,256,512]{2,1,0:T(8,128)}) custom-call(s32[4,32]{1,0:T(4,128)} %band_hbm.1, s32[4]{0:T(128)} %id_hbm.1, f32[1,128]{1,0:T(1,128)} %bitcast.3, f32[4,2,128,512]{3,2,1,0:T(8,128)} %upd_hbm.1, bf16[4,32,256,128]{3,2,1,0:T(8,128)(2,1)} %tiles_hbm.1, f32[128,2,128]{2,1,0:T(2,128)} %vol_hbm.1), custom_call_target="tpu_custom_call" | custom-call | tf_op jit(solution)/shard_map/exchange/pallas_call | solution.py:391
  58.2 1.6 %copy.10 = f32[128,2,128]{2,1,0:T(2,128)} copy(f32[128,2,128]{2,1,0:T(2,128)} %get-tuple-element.8) | data formatting | bytes 262144
  59.8 3.1 %copy.11 = f32[4,2,128,512]{3,2,1,0:T(8,128)} copy(f32[4,2,128,512]{3,2,1,0:T(8,128)} %bitcast.2) | data formatting | bytes 4194304

commit v3 on v2

--- a/solution.py
+++ b/solution.py
@@ -45,7 +45,7 @@
     tiles_hbm,
     vol_hbm,
     vnext_ref,
-    out_ref,
+    out_hbm,
     band_ref,
     id_ref,
     weight_ref,
@@ -66,6 +66,8 @@
     rz,
     gath,
     acc,
+    outs,
+    out_sem,
     in_sem,
     tile_sem,
     halo_ss,
@@ -150,8 +152,6 @@
 
     def one_tile(c, ty, th, tx):
         j = ty * (NH * NX) + th * NX + tx
-        if c == 0:
-            tile_copy(ty, th, tx).wait()
         windows = [scaled[c, 3 * a + band_ref[a, j]] for a in range(ANG)]
         total = jnp.dot(
             jnp.concatenate(windows, axis=1),
@@ -161,6 +161,15 @@
         part[ty, th, tx, rows(c), :] = total.astype(BF)
 
     def back(c, d):
+        if c == 0:
+
+            def arrive(i, carry):
+                tile_copy(i, 0, xs[d]).wait()
+                tile_copy(ys[d], 1, i).wait()
+                return carry
+
+            lax.fori_loop(0, 4, arrive, 0)
+
         def body(i, carry):
             for u in range(2):
                 one_tile(c, 2 * i + u, 0, xs[d])
@@ -276,6 +285,7 @@
             gath[y, path, x, :, rows(c)] = field.astype(BF)
             for d in FAR:
                 gather1(path, c, d).start()
+        for path in range(2):
             for d in FAR:
                 gather2(path, c, d, 0).start()
         vnext_ref[:, c, :] = jnp.where(h == 0, fields[0], fields[1])
@@ -287,18 +297,17 @@
                 for d in FAR:
                     gather2(path, c, d, k).start()
 
-    def project(c, d, begin, end):
-        tx, ty = xs[(4 - d) % 4], ys[(4 - d) % 4]
-        if d:
+    def project(c, k, begin, end):
+        if k is None:
+            places = [(i, 0, x) for i in range(4)] + [(y, 1, i) for i in range(4)]
+        else:
             for path in range(2):
-                for k in range(4):
+                for d in (1, 2, 3):
                     gather2(path, c, d, k).wait_recv()
-        right = jnp.concatenate(
-            [gath[i, 0, tx, :, rows(c)] for i in range(4)]
-            + [gath[ty, 1, i, :, rows(c)] for i in range(4)],
-            axis=0,
-        )
-        picks = [i * 8 + tx for i in range(4)] + [ty * 8 + 4 + i for i in range(4)]
+            places = [(ys[(4 - k) % 4], 0, xs[d]) for d in (1, 2, 3)]
+            places += [(ys[d], 1, xs[(4 - k) % 4]) for d in (1, 2, 3)]
+        right = jnp.concatenate([gath[ty, th, tx, :, rows(c)] for ty, th, tx in places], axis=0)
+        picks = [ty * 8 + th * 4 + tx for ty, th, tx in places]
 
         def body(g, carry):
             for u in range(2):
@@ -310,12 +319,19 @@
                 if not begin:
                     term = term + acc[c, a]
                 if end:
-                    out_ref[a, rows(c), :] = term.T
+                    outs[a, rows(c), :] = term.T
                 else:
                     acc[c, a] = term
             return carry
 
         lax.fori_loop(0, 2, body, 0)
+        if end:
+            out_copy(c).start()
+
+    def out_copy(c):
+        return pltpu.make_async_copy(
+            outs.at[:, rows(c), :], out_hbm.at[:, rows(c), :], out_sem.at[c]
+        )
 
     scale(0)
     band_copy.wait()
@@ -324,18 +340,18 @@
     for c in range(2):
         vt[c] = vol_ref[:, c, :].T
     pl.semaphore_wait(barrier, len(peers))
+    send_first(0, 2)
     for c in range(2):
         halo_copy(c, 0).start()
         halo_copy(c, 1).start()
-    send_first(0, 2)
     back(0, 1)
     send_first(0, 1)
     back(0, 3)
     send_first(0, 3)
-    back(0, 0)
     scale(1)
     back(1, 2)
     send_first(1, 2)
+    back(0, 0)
     for c in range(2):
         halo_copy(c, 0).wait_recv()
         halo_copy(c, 1).wait_recv()
@@ -348,27 +364,31 @@
         smooth[c] = mid - SMOOTHING * (2.0 * mid - before - after)
     smooth_copy.start()
     back(1, 1)
+    back(1, 3)
+    back(1, 0)
+    sum_first(0)
     send_first(1, 1)
-    back(1, 3)
-    sum_first(0)
     send_first(1, 3)
-    back(1, 0)
     sum_second(0)
     sum_first(1)
     smooth_copy.wait_recv()
     finish_volume(0)
     sum_second(1)
     relay(0)
-    project(0, 0, True, False)
+    project(0, None, True, False)
+    project(0, 0, False, False)
     finish_volume(1)
-    relay(1)
     project(0, 1, False, False)
     project(0, 3, False, False)
+    relay(1)
     project(0, 2, False, True)
-    project(1, 0, True, False)
+    project(1, None, True, False)
+    project(1, 0, False, False)
     project(1, 1, False, False)
     project(1, 3, False, False)
     project(1, 2, False, True)
+    out_copy(0).wait()
+    out_copy(1).wait()
 
     smooth_copy.wait_send()
     for c in range(2):
@@ -384,6 +404,20 @@
                     gather2(path, c, d, k).wait_send()
 
 
+def deliver_kernel(small_in, large_in, small_out, large_out, small, large, sems):
+    pairs = [(small_in, small, small_out)]
+    pairs += [(large_in.at[i], large.at[i], large_out.at[i]) for i in range(large.shape[0])]
+    loads = [pltpu.make_async_copy(a, b, sems.at[0, i]) for i, (a, b, c) in enumerate(pairs)]
+    stores = [pltpu.make_async_copy(b, c, sems.at[1, i]) for i, (a, b, c) in enumerate(pairs)]
+    for load in loads:
+        load.start()
+    for load, store in zip(loads, stores):
+        load.wait()
+        store.start()
+    for store in stores:
+        store.wait()
+
+
 def shards(updates, interp_tiles, band_start, angle_id, angle_weight, volume):
     vmem = pl.BlockSpec(memory_space=pltpu.VMEM)
     hbm = pl.BlockSpec(memory_space=pl.ANY)
@@ -395,7 +429,7 @@
             jax.ShapeDtypeStruct((4, 256, 512), F32),
         ),
         in_specs=[hbm] * 6,
-        out_specs=(vmem, vmem),
+        out_specs=(vmem, hbm),
         scratch_shapes=[
             pltpu.SMEM((4, 32), jnp.int32),
             pltpu.SMEM((4,), jnp.int32),
@@ -417,6 +451,8 @@
             pltpu.VMEM((2, 2, 128, 128), BF),
             pltpu.VMEM((4, 2, 4, 128, 256), BF),
             pltpu.VMEM((2, 4, 512, 128), F32),
+            pltpu.VMEM((4, 256, 512), F32),
+            dma((2,)),
             dma((6,)),
             dma((32,)),
             dma((2, 2)),
@@ -439,6 +475,22 @@
         ),
         name="exchange",
     )(band_start, angle_id, angle_weight.reshape(1, 128), updates, interp_tiles, volume)
+    vnext, projection = pl.pallas_call(
+        deliver_kernel,
+        out_shape=(
+            jax.ShapeDtypeStruct((128, 2, 128), F32),
+            jax.ShapeDtypeStruct((8, 128, 512), F32),
+        ),
+        in_specs=[hbm] * 2,
+        out_specs=(hbm, hbm),
+        scratch_shapes=[
+            pltpu.VMEM((128, 2, 128), F32),
+            pltpu.VMEM((8, 128, 512), F32),
+            dma((2, 9)),
+        ],
+        compiler_params=pltpu.CompilerParams(vmem_limit_bytes=63 * 2**20),
+        name="deliver",
+    )(vnext, projection.reshape(8, 128, 512))
     return vnext, projection.reshape(4, 2, 128, 512)
 
 

time: 63.3 us -> 54.7 us (0.86)
  local copies, waits for them, and re-layouts: 4.65 us -> 0 us
  Pallas kernels: 57.5 us -> 53.9 us
    pallas_call x1, Pallas kernels: 57.5 us -> 51.4 us  [shards(): pl.pallas_call(whole_kernel, out_shape=(jax.ShapeDtypeStruct((128, 2, 128...]
    unnamed x2 -> x0, local copies, waits for them, and re-layouts: 4.65 us -> none
    pallas_call x0 -> x1, Pallas kernels: none -> 2.48 us  [shards(): pl.pallas_call(deliver_kernel, out_shape=(jax.ShapeDtypeStruct((128, 2, 1...]
where the time goes in v3:
time: 54.7 us; the launch traced here: 54.5 us
  Pallas kernels  53.9 us (99%)
  between operations  0.64 us (1%)
    pallas_call x1, Pallas kernels, shards(): pl.pallas_call(whole_kernel, out_shape=(jax.ShapeDtypeStruct((128, 2, 128...  51.4 us
    pallas_call x1, Pallas kernels, shards(): pl.pallas_call(deliver_kernel, out_shape=(jax.ShapeDtypeStruct((128, 2, 1...  2.48 us

profile of v3, /device:TPU:2, one launch (start us, length us, event | category | flops | bytes accessed | tf_op | source)
XLA Modules:
  0.0 54.5 jit_solution(9344778025002602432)
XLA Ops:
  0.6 51.4 %exchange.1 = (f32[128,2,128]{2,1,0:T(2,128)}, f32[4,256,512]{2,1,0:T(8,128)}) custom-call(s32[4,32]{1,0:T(4,128)} %band_hbm.1, s32[4]{0:T(128)} %id_hbm.1, f32[1,128]{1,0:T(1,128)} %bitcast.4, f32[4,2,128,512]{3,2,1,0:T(8,128)} %upd_hbm.1, bf16[4,32,256,128]{3,2,1,0:T(8,128)(2,1)} %tiles_hbm.1, f32[128,2,128]{2,1,0:T(2,128)} %vol_hbm.1), custom_call_target="tpu_custom_call" | custom-call | tf_op jit(solution)/shard_map/exchange/pallas_call | solution.py:425
  52.1 2.5 %deliver.1 = (f32[128,2,128]{2,1,0:T(2,128)}, f32[8,128,512]{2,1,0:T(8,128)}) custom-call(f32[128,2,128]{2,1,0:T(2,128)} %get-tuple-element.6.small_in, f32[8,128,512]{2,1,0:T(8,128)} %bitcast.3), custom_call_target="tpu_custom_call" | custom-call | tf_op jit(solution)/shard_map/deliver/pallas_call | solution.py:478

commit v4 on v3

--- a/solution.py
+++ b/solution.py
@@ -58,6 +58,8 @@
     halo,
     smooth,
     smooth_in,
+    rr,
+    both,
     r1,
     s2,
     r2,
@@ -74,8 +76,8 @@
     halo_rs,
     sm_ss,
     sm_rs,
-    ss1,
-    rs1,
+    trs,
+    trr,
     ss2,
     rs2,
     zss,
@@ -188,14 +190,60 @@
             device_id_type=MESH,
         )
 
-    def first(path, c, d):
+    def part_of(path, c, d, half):
+        two = slice(2 * half, 2 * half + 2)
         if path == 0:
-            src, where = part.at[:, 0, xs[d], rows(c), :], device(xs[d], y, h, s)
-        else:
-            src, where = part.at[ys[d], 1, :, rows(c), :], device(x, ys[d], h, s)
+            return part.at[two, 0, xs[d], rows(c), :]
+        return part.at[ys[d], 1, two, rows(c), :]
+
+    def step_to(path, side):
+        d = 1 if side else 3
+        return device(xs[d], y, h, s) if path == 0 else device(x, ys[d], h, s)
+
+    def through(path, c, side):
         return remote(
-            src, r1.at[path, c, d - 1], ss1.at[path, c, d - 1], rs1.at[path, c, d - 1], where
-        )
+            part_of(path, c, 2, side),
+            rr.at[path, c, side],
+            trs.at[0, path, c, side],
+            trr.at[0, path, c, side],
+            step_to(path, side),
+        )
+
+    def direct(path, c, side):
+        half = 1 - side
+        return remote(
+            part_of(path, c, 1 if side else 3, half),
+            r1.at[path, c, 0, half],
+            trs.at[1, path, c, side],
+            trr.at[1, path, c, side],
+            step_to(path, side),
+        )
+
+    def joined(path, c, side):
+        return remote(
+            both.at[path, c, side],
+            r1.at[path, c, 1, side],
+            trs.at[2, path, c, side],
+            trr.at[2, path, c, side],
+            step_to(path, side),
+        )
+
+    def join(c):
+        for path in range(2):
+            for side in range(2):
+                through(path, c, side).wait_recv()
+                own = part_of(path, c, 1 if side else 3, side)[...].astype(F32)
+                both[path, c, side] = (own + rr[path, c, side].astype(F32)).astype(BF)
+                joined(path, c, side).start()
+
+    def send_through(c):
+        for side in range(2):
+            for path in range(2):
+                through(path, c, side).start()
+
+    def send_direct(c, side):
+        for path in range(2):
+            direct(path, c, side).start()
 
     def inner(path, d):
         return device(x, ys[d], h, s) if path == 0 else device(xs[d], y, h, s)
@@ -241,20 +289,17 @@
 
     smooth_copy = remote(smooth, smooth_in, sm_ss, sm_rs, device(x, y, 1 - h, s))
 
-    def send_first(c, d):
-        first(0, c, d).start()
-        first(1, c, d).start()
-
     def sum_first(c):
         for path in range(2):
-            for d in (1, 2, 3):
-                first(path, c, d).wait_recv()
+            for side in range(2):
+                direct(path, c, side).wait_recv()
+                joined(path, c, side).wait_recv()
             for d in FAR + (0,):
                 at = ys[d] if path == 0 else xs[d]
                 own = part[at, 0, x, rows(c), :] if path == 0 else part[y, 1, at, rows(c), :]
                 total = own.astype(F32)
-                for k in range(3):
-                    total = total + r1[path, c, k, at].astype(F32)
+                for k in range(2):
+                    total = total + r1[path, c, k, at // 2, lax.rem(at, 2)].astype(F32)
                 if d:
                     s2[path, c, d - 1] = total.astype(BF)
                     second(path, c, d).start()
@@ -285,53 +330,50 @@
             gath[y, path, x, :, rows(c)] = field.astype(BF)
             for d in FAR:
                 gather1(path, c, d).start()
-        for path in range(2):
-            for d in FAR:
-                gather2(path, c, d, 0).start()
         vnext_ref[:, c, :] = jnp.where(h == 0, fields[0], fields[1])
 
-    def relay(c):
-        for k in (1, 3, 2):
+    def spread(path, c, k):
+        for d in FAR:
+            gather2(path, c, d, k).start()
+
+    def send_own(c):
+        for path in range(2):
+            spread(path, c, 0)
+
+    def relay(c, order=(1, 3, 2)):
+        for k in order:
             for path in range(2):
                 gather1(path, c, k).wait_recv()
-                for d in FAR:
-                    gather2(path, c, d, k).start()
-
-    def project(c, k, begin, end):
+                spread(path, c, k)
+
+    def project(channels, k, begin, end):
         if k is None:
             places = [(i, 0, x) for i in range(4)] + [(y, 1, i) for i in range(4)]
         else:
             for path in range(2):
-                for d in (1, 2, 3):
-                    gather2(path, c, d, k).wait_recv()
+                for c in channels:
+                    for d in FAR:
+                        gather2(path, c, d, k).wait_recv()
             places = [(ys[(4 - k) % 4], 0, xs[d]) for d in (1, 2, 3)]
             places += [(ys[d], 1, xs[(4 - k) % 4]) for d in (1, 2, 3)]
-        right = jnp.concatenate([gath[ty, th, tx, :, rows(c)] for ty, th, tx in places], axis=0)
+        cols = slice(channels[0] * 128, channels[-1] * 128 + 128)
+        right = jnp.concatenate([gath[ty, th, tx, :, cols] for ty, th, tx in places], axis=0)
         picks = [ty * 8 + th * 4 + tx for ty, th, tx in places]
-
-        def body(g, carry):
-            for u in range(2):
-                a = 2 * g + u
-                left = jnp.concatenate(
-                    [placed_rows(tiles[j, a], band_ref[a, j]) for j in picks], axis=1
-                )
-                term = jnp.dot(left, right, preferred_element_type=F32)
-                if not begin:
-                    term = term + acc[c, a]
-                if end:
-                    outs[a, rows(c), :] = term.T
-                else:
-                    acc[c, a] = term
-            return carry
-
-        lax.fori_loop(0, 2, body, 0)
-        if end:
-            out_copy(c).start()
-
-    def out_copy(c):
-        return pltpu.make_async_copy(
-            outs.at[:, rows(c), :], out_hbm.at[:, rows(c), :], out_sem.at[c]
-        )
+        for a in range(ANG):
+            left = jnp.concatenate(
+                [placed_rows(tiles[j, a], band_ref[a, j]) for j in picks], axis=1
+            )
+            term = jnp.dot(left, right, preferred_element_type=F32)
+            if not begin:
+                term = term + acc[a, :, cols]
+            if end:
+                outs[a, cols, :] = term.T
+                out_copy(a).start()
+            else:
+                acc[a, :, cols] = term
+
+    def out_copy(a):
+        return pltpu.make_async_copy(outs.at[a], out_hbm.at[a], out_sem.at[a])
 
     scale(0)
     band_copy.wait()
@@ -340,17 +382,17 @@
     for c in range(2):
         vt[c] = vol_ref[:, c, :].T
     pl.semaphore_wait(barrier, len(peers))
-    send_first(0, 2)
+    send_through(0)
     for c in range(2):
         halo_copy(c, 0).start()
         halo_copy(c, 1).start()
     back(0, 1)
-    send_first(0, 1)
+    send_direct(0, 1)
     back(0, 3)
-    send_first(0, 3)
+    send_direct(0, 0)
     scale(1)
     back(1, 2)
-    send_first(1, 2)
+    send_through(1)
     back(0, 0)
     for c in range(2):
         halo_copy(c, 0).wait_recv()
@@ -363,32 +405,33 @@
         after = jnp.where(row == 127, high, pltpu.roll(mid, 127, 0))
         smooth[c] = mid - SMOOTHING * (2.0 * mid - before - after)
     smooth_copy.start()
+    join(0)
     back(1, 1)
+    send_direct(1, 1)
     back(1, 3)
+    send_direct(1, 0)
     back(1, 0)
+    join(1)
     sum_first(0)
-    send_first(1, 1)
-    send_first(1, 3)
+    sum_first(1)
     sum_second(0)
-    sum_first(1)
+    sum_second(1)
     smooth_copy.wait_recv()
     finish_volume(0)
-    sum_second(1)
+    send_own(0)
+    finish_volume(1)
     relay(0)
-    project(0, None, True, False)
-    project(0, 0, False, False)
-    finish_volume(1)
-    project(0, 1, False, False)
-    project(0, 3, False, False)
+    send_own(1)
+    project((0,), None, True, False)
     relay(1)
-    project(0, 2, False, True)
-    project(1, None, True, False)
-    project(1, 0, False, False)
-    project(1, 1, False, False)
-    project(1, 3, False, False)
-    project(1, 2, False, True)
-    out_copy(0).wait()
-    out_copy(1).wait()
+    project((1,), None, True, False)
+    project((0,), 0, False, False)
+    project((1,), 0, False, False)
+    project((0, 1), 1, False, False)
+    project((0, 1), 3, False, False)
+    project((0, 1), 2, False, True)
+    for a in range(ANG):
+        out_copy(a).wait()
 
     smooth_copy.wait_send()
     for c in range(2):
@@ -396,11 +439,15 @@
         halo_copy(c, 1).wait_send()
         for path in range(2):
             across(path, c).wait_send()
+            for side in range(2):
+                through(path, c, side).wait_send()
+                direct(path, c, side).wait_send()
+                joined(path, c, side).wait_send()
             for d in (1, 2, 3):
-                first(path, c, d).wait_send()
                 second(path, c, d).wait_send()
                 gather1(path, c, d).wait_send()
-                for k in range(4):
+            for k in range(4):
+                for d in FAR:
                     gather2(path, c, d, k).wait_send()
 
 
@@ -443,24 +490,26 @@
             pltpu.VMEM((2, 2, 8, 128), F32),
             pltpu.VMEM((2, 128, 128), F32),
             pltpu.VMEM((2, 128, 128), F32),
-            pltpu.VMEM((2, 2, 3, 4, 128, 128), BF),
+            pltpu.VMEM((2, 2, 2, 2, 128, 128), BF),
+            pltpu.VMEM((2, 2, 2, 2, 128, 128), BF),
+            pltpu.VMEM((2, 2, 2, 2, 2, 128, 128), BF),
             pltpu.VMEM((2, 2, 3, 128, 128), BF),
             pltpu.VMEM((2, 2, 3, 128, 128), BF),
             pltpu.VMEM((2, 2, 128, 128), F32),
             pltpu.VMEM((2, 2, 128, 128), BF),
             pltpu.VMEM((2, 2, 128, 128), BF),
             pltpu.VMEM((4, 2, 4, 128, 256), BF),
-            pltpu.VMEM((2, 4, 512, 128), F32),
+            pltpu.VMEM((4, 512, 256), F32),
             pltpu.VMEM((4, 256, 512), F32),
-            dma((2,)),
+            dma((4,)),
             dma((6,)),
             dma((32,)),
             dma((2, 2)),
             dma((2, 2)),
             dma,
             dma,
-            dma((2, 2, 3)),
-            dma((2, 2, 3)),
+            dma((3, 2, 2, 2)),
+            dma((3, 2, 2, 2)),
             dma((2, 2, 3)),
             dma((2, 2, 3)),
             dma((2, 2)),

time: 54.7 us -> 53.8 us (0.984)
  Pallas kernels: 53.9 us -> 52.7 us
    pallas_call x1, Pallas kernels: 51.4 us -> 50.2 us  [shards(): pl.pallas_call(whole_kernel, out_shape=(jax.ShapeDtypeStruct((128, 2, 128...]
where the time goes in v4:
time: 53.8 us; the launch traced here: 53.5 us
  Pallas kernels  52.7 us (98%)
  between operations  0.8 us (1%)
    pallas_call x1, Pallas kernels, shards(): pl.pallas_call(whole_kernel, out_shape=(jax.ShapeDtypeStruct((128, 2, 128...  50.2 us
    pallas_call x1, Pallas kernels, shards(): pl.pallas_call(deliver_kernel, out_shape=(jax.ShapeDtypeStruct((128, 2, 1...  2.48 us

profile of v4, /device:TPU:2, one launch (start us, length us, event | category | flops | bytes accessed | tf_op | source)
XLA Modules:
  0.0 53.5 jit_solution(1051656579295650315)
XLA Ops:
  0.6 50.2 %exchange.1 = (f32[128,2,128]{2,1,0:T(2,128)}, f32[4,256,512]{2,1,0:T(8,128)}) custom-call(s32[4,32]{1,0:T(4,128)} %band_hbm.1, s32[4]{0:T(128)} %id_hbm.1, f32[1,128]{1,0:T(1,128)} %bitcast.4, f32[4,2,128,512]{3,2,1,0:T(8,128)} %upd_hbm.1, bf16[4,32,256,128]{3,2,1,0:T(8,128)(2,1)} %tiles_hbm.1, f32[128,2,128]{2,1,0:T(2,128)} %vol_hbm.1), custom_call_target="tpu_custom_call" | custom-call | tf_op jit(solution)/shard_map/exchange/pallas_call | solution.py:472
  50.9 2.5 %deliver.1 = (f32[128,2,128]{2,1,0:T(2,128)}, f32[8,128,512]{2,1,0:T(8,128)}) custom-call(f32[128,2,128]{2,1,0:T(2,128)} %get-tuple-element.6.small_in, f32[8,128,512]{2,1,0:T(8,128)} %bitcast.3), custom_call_target="tpu_custom_call" | custom-call | tf_op jit(solution)/shard_map/deliver/pallas_call | solution.py:527

commit v5 on v4

--- a/solution.py
+++ b/solution.py
@@ -162,7 +162,7 @@
         )
         part[ty, th, tx, rows(c), :] = total.astype(BF)
 
-    def back(c, d):
+    def back(c, d, begin=0, end=2):
         if c == 0:
 
             def arrive(i, carry):
@@ -170,7 +170,7 @@
                 tile_copy(ys[d], 1, i).wait()
                 return carry
 
-            lax.fori_loop(0, 4, arrive, 0)
+            lax.fori_loop(2 * begin, 2 * end, arrive, 0)
 
         def body(i, carry):
             for u in range(2):
@@ -178,7 +178,7 @@
                 one_tile(c, ys[d], 1, 2 * i + u)
             return carry
 
-        lax.fori_loop(0, 2, body, 0)
+        lax.fori_loop(begin, end, body, 0)
 
     def remote(src, dst, send, recv, where):
         return pltpu.make_async_remote_copy(
@@ -236,10 +236,9 @@
                 both[path, c, side] = (own + rr[path, c, side].astype(F32)).astype(BF)
                 joined(path, c, side).start()
 
-    def send_through(c):
-        for side in range(2):
-            for path in range(2):
-                through(path, c, side).start()
+    def send_through(c, side):
+        for path in range(2):
+            through(path, c, side).start()
 
     def send_direct(c, side):
         for path in range(2):
@@ -377,12 +376,14 @@
 
     scale(0)
     band_copy.wait()
-    back(0, 2)
+    back(0, 2, 0, 1)
+    pl.semaphore_wait(barrier, len(peers))
+    send_through(0, 0)
+    back(0, 2, 1, 2)
+    send_through(0, 1)
     vol_copy.wait()
     for c in range(2):
         vt[c] = vol_ref[:, c, :].T
-    pl.semaphore_wait(barrier, len(peers))
-    send_through(0)
     for c in range(2):
         halo_copy(c, 0).start()
         halo_copy(c, 1).start()
@@ -392,7 +393,8 @@
     send_direct(0, 0)
     scale(1)
     back(1, 2)
-    send_through(1)
+    send_through(1, 0)
+    send_through(1, 1)
     back(0, 0)
     for c in range(2):
         halo_copy(c, 0).wait_recv()

time: 53.8 us -> 52.5 us (0.976)
  Pallas kernels: 52.7 us -> 51.5 us
    pallas_call x1, Pallas kernels: 50.2 us -> 49.1 us  [shards(): pl.pallas_call(whole_kernel, out_shape=(jax.ShapeDtypeStruct((128, 2, 128...]
where the time goes in v5:
time: 52.5 us; the launch traced here: 52.3 us
  Pallas kernels  51.5 us (98%)
  between operations  0.8 us (2%)
    pallas_call x1, Pallas kernels, shards(): pl.pallas_call(whole_kernel, out_shape=(jax.ShapeDtypeStruct((128, 2, 128...  49.1 us
    pallas_call x1, Pallas kernels, shards(): pl.pallas_call(deliver_kernel, out_shape=(jax.ShapeDtypeStruct((128, 2, 1...  2.48 us

profile of v5, /device:TPU:2, one launch (start us, length us, event | category | flops | bytes accessed | tf_op | source)
XLA Modules:
  0.0 52.3 jit_solution(7605733239403194663)
XLA Ops:
  0.6 49.1 %exchange.1 = (f32[128,2,128]{2,1,0:T(2,128)}, f32[4,256,512]{2,1,0:T(8,128)}) custom-call(s32[4,32]{1,0:T(4,128)} %band_hbm.1, s32[4]{0:T(128)} %id_hbm.1, f32[1,128]{1,0:T(1,128)} %bitcast.4, f32[4,2,128,512]{3,2,1,0:T(8,128)} %upd_hbm.1, bf16[4,32,256,128]{3,2,1,0:T(8,128)(2,1)} %tiles_hbm.1, f32[128,2,128]{2,1,0:T(2,128)} %vol_hbm.1), custom_call_target="tpu_custom_call" | custom-call | tf_op jit(solution)/shard_map/exchange/pallas_call | solution.py:474
  49.7 2.5 %deliver.1 = (f32[128,2,128]{2,1,0:T(2,128)}, f32[8,128,512]{2,1,0:T(8,128)}) custom-call(f32[128,2,128]{2,1,0:T(2,128)} %get-tuple-element.6.small_in, f32[8,128,512]{2,1,0:T(8,128)} %bitcast.3), custom_call_target="tpu_custom_call" | custom-call | tf_op jit(solution)/shard_map/deliver/pallas_call | solution.py:529

commit v6 on v5

--- a/solution.py
+++ b/solution.py
@@ -329,7 +329,7 @@
             gath[y, path, x, :, rows(c)] = field.astype(BF)
             for d in FAR:
                 gather1(path, c, d).start()
-        vnext_ref[:, c, :] = jnp.where(h == 0, fields[0], fields[1])
+        smooth[c] = jnp.where(h == 0, fields[0], fields[1])
 
     def spread(path, c, k):
         for d in FAR:
@@ -418,14 +418,16 @@
     sum_first(1)
     sum_second(0)
     sum_second(1)
-    smooth_copy.wait_recv()
+    smooth_copy.wait()
     finish_volume(0)
     send_own(0)
     finish_volume(1)
+    send_own(1)
     relay(0)
-    send_own(1)
     project((0,), None, True, False)
     relay(1)
+    for c in range(2):
+        vnext_ref[:, c, :] = smooth[c]
     project((1,), None, True, False)
     project((0,), 0, False, False)
     project((1,), 0, False, False)
@@ -435,7 +437,6 @@
     for a in range(ANG):
         out_copy(a).wait()
 
-    smooth_copy.wait_send()
     for c in range(2):
         halo_copy(c, 0).wait_send()
         halo_copy(c, 1).wait_send()

time: 52.5 us -> 52.2 us (level)
  no operation moved by 1% of the time
where the time goes in v6:
time: 52.2 us; the launch traced here: 52.1 us
  Pallas kernels  51.3 us (98%)
  between operations  0.8 us (2%)
    pallas_call x1, Pallas kernels, shards(): pl.pallas_call(whole_kernel, out_shape=(jax.ShapeDtypeStruct((128, 2, 128...  48.8 us
    pallas_call x1, Pallas kernels, shards(): pl.pallas_call(deliver_kernel, out_shape=(jax.ShapeDtypeStruct((128, 2, 1...  2.48 us

profile of v6, /device:TPU:2, one launch (start us, length us, event | category | flops | bytes accessed | tf_op | source)
XLA Modules:
  0.0 52.1 jit_solution(9488401535290649242)
XLA Ops:
  0.6 48.8 %exchange.1 = (f32[128,2,128]{2,1,0:T(2,128)}, f32[4,256,512]{2,1,0:T(8,128)}) custom-call(s32[4,32]{1,0:T(4,128)} %band_hbm.1, s32[4]{0:T(128)} %id_hbm.1, f32[1,128]{1,0:T(1,128)} %bitcast.4, f32[4,2,128,512]{3,2,1,0:T(8,128)} %upd_hbm.1, bf16[4,32,256,128]{3,2,1,0:T(8,128)(2,1)} %tiles_hbm.1, f32[128,2,128]{2,1,0:T(2,128)} %vol_hbm.1), custom_call_target="tpu_custom_call" | custom-call | tf_op jit(solution)/shard_map/exchange/pallas_call | solution.py:475
  49.4 2.5 %deliver.1 = (f32[128,2,128]{2,1,0:T(2,128)}, f32[8,128,512]{2,1,0:T(8,128)}) custom-call(f32[128,2,128]{2,1,0:T(2,128)} %get-tuple-element.6.small_in, f32[8,128,512]{2,1,0:T(8,128)} %bitcast.3), custom_call_target="tpu_custom_call" | custom-call | tf_op jit(solution)/shard_map/deliver/pallas_call | solution.py:530
